TPU v7x, 32 devices: a whole 2x2x4 slice. The times are simulated.
32 devices in a mesh: gx: 8 (over z, y), gy: 4 (over x, core).
Axes of the slice: x: 2, y: 2, z: 4, core: 2. Of those that a mesh axis runs over, the one named last changes fastest.
Arguments:
- tokens: bfloat16 [256, 8192], P('gy', 'gx'), may hold values from -6 to 6
- target: bfloat16 [256, 8192], P('gy', 'gx'), may hold values from -6 to 6
- w_gate: bfloat16 [8192, 14336], P('gx', 'gy'), may hold values from -0.0625 to 0.0625
- w_up: bfloat16 [8192, 14336], P('gx', 'gy'), may hold values from -0.0625 to 0.0625
- w_down: bfloat16 [14336, 8192], P('gy', 'gx'), may hold values from -0.046875 to 0.046875
- t_gate: bfloat16 [8192, 14336], P('gx', 'gy'), may hold values from -0.0625 to 0.0625
- t_up: bfloat16 [8192, 14336], P('gx', 'gy'), may hold values from -0.0625 to 0.0625
- t_down: bfloat16 [14336, 8192], P('gy', 'gx'), may hold values from -0.046875 to 0.046875
Outputs:
- hvp_gate: bfloat16 [8192, 14336], P('gx', 'gy')
- hvp_up: bfloat16 [8192, 14336], P('gx', 'gy')
- hvp_down: bfloat16 [14336, 8192], P('gy', 'gx')
All inputs are finite; a program needn't handle non-finite values.
Results may differ from a plain program's by a relative error of at most 0.0074.
Values may be sent and summed in bfloat16 or wider, within the bound.
A program may use at most 192 MiB of HBM per device.

v0:
```python
import math

import jax
import jax.numpy as jnp
from jax import lax
from jax.sharding import PartitionSpec as P

TOKENS = 256


def silu_parts(gate):
    sig = jax.nn.sigmoid(gate)
    first = sig * (1.0 + gate * (1.0 - sig))
    second = sig * (1.0 - sig) * (2.0 + gate * (1.0 - 2.0 * sig))
    return (gate * sig, first, second)


def matmul(left, right):
    return jnp.dot(left, right, preferred_element_type=jnp.float32)


def lead_dot(left, right):
    return lax.dot_general(
        left, right, (((0,), (0,)), ((), ())), preferred_element_type=jnp.float32
    )


def tail_dot(left, right):
    return lax.dot_general(
        left, right, (((1,), (1,)), ((), ())), preferred_element_type=jnp.float32
    )


def body(tokens, target, w_gate, w_up, w_down, t_gate, t_up, t_down):
    scale = 1.0 / math.sqrt(TOKENS)
    width = w_gate.shape[1]
    dlocal = w_down.shape[1]
    xfull = lax.all_gather(tokens, "gy", axis=0, tiled=True)
    w_joined = jnp.concatenate([w_gate, w_up, t_gate, t_up], 1)
    rows = xfull
    summed = lax.psum_scatter(matmul(rows, w_joined), "gx", scatter_dimension=0, tiled=True)
    gate = summed[:, :width]
    upper = summed[:, width : 2 * width]
    gate_dot = summed[:, 2 * width : 3 * width]
    upper_dot = summed[:, 3 * width :]
    silu_val, first, second = silu_parts(gate)
    hidden = (silu_val * upper).astype(jnp.bfloat16)
    hidden_dot = (first * gate_dot * upper + silu_val * upper_dot).astype(jnp.bfloat16)
    hid_full, hid_dot_full = (
        lax.all_gather(hidden, "gx", axis=0, tiled=True),
        lax.all_gather(hidden_dot, "gx", axis=0, tiled=True),
    )
    rows = hid_full
    rows_dot = hid_dot_full
    output = matmul(rows, w_down)
    output_dot = matmul(rows_dot, w_down) + matmul(rows, t_down)
    outputs = lax.psum_scatter(
        jnp.concatenate([output, output_dot], 1), "gy", scatter_dimension=0, tiled=True
    )
    grad = ((outputs[:, :dlocal] - target.astype(jnp.float32)) * scale).astype(jnp.bfloat16)
    grad_dot = (outputs[:, dlocal:] * scale).astype(jnp.bfloat16)
    grad_full, grad_dot_full = (
        lax.all_gather(grad, "gy", axis=0, tiled=True),
        lax.all_gather(grad_dot, "gy", axis=0, tiled=True),
    )
    hvp_down = (lead_dot(hid_dot_full, grad_full) + lead_dot(hid_full, grad_dot_full)).astype(
        jnp.bfloat16
    )
    rows = grad_full
    rows_dot = grad_dot_full
    back = tail_dot(rows, w_down)
    back_dot = tail_dot(rows_dot, w_down) + tail_dot(rows, t_down)
    backs = lax.psum_scatter(
        jnp.concatenate([back, back_dot], 1), "gx", scatter_dimension=0, tiled=True
    )
    back = backs[:, :width]
    back_dot = backs[:, width:]
    gate_in = (
        back_dot * upper * first + back * upper_dot * first + back * upper * second * gate_dot
    ).astype(jnp.bfloat16)
    upper_in = (back_dot * silu_val + back * first * gate_dot).astype(jnp.bfloat16)
    gate_full, upper_full = (
        lax.all_gather(gate_in, "gx", axis=0, tiled=True),
        lax.all_gather(upper_in, "gx", axis=0, tiled=True),
    )
    hvp_gate = lead_dot(xfull, gate_full).astype(jnp.bfloat16)
    hvp_up = lead_dot(xfull, upper_full).astype(jnp.bfloat16)
    return (hvp_gate, hvp_up, hvp_down)


def solution(mesh):
    return jax.shard_map(
        body,
        mesh=mesh,
        in_specs=(
            P("gy", "gx"),
            P("gy", "gx"),
            P("gx", "gy"),
            P("gx", "gy"),
            P("gy", "gx"),
            P("gx", "gy"),
            P("gx", "gy"),
            P("gy", "gx"),
        ),
        out_specs=(P("gx", "gy"), P("gx", "gy"), P("gy", "gx")),
        check_vma=False,
    )
```

profile of v0, /device:TPU:0, one launch (start us, length us, event | category | flops | bytes accessed | tf_op | source)
XLA Modules:
  0.0 711.9 jit_solution(17920189358858939626)
XLA Ops:
  7.2 8.9 %all_gather.21 = bf16[256,1024]{1,0:T(8,128)(2,1)S(1)} all-gather(bf16[64,1024]{1,0:T(8,128)(2,1)} %param.8), channel_id=1, replica_groups=mesh['gx'=8,'gy'=4] {'gy'}, dimensions={0}, use_global_device_ids=true | all-gather | bytes 655360 | tf_op jit(solution)/shard_map/all_gather | solution.py:38
  16.1 20.4 %fusion.8 = f32[256,14336]{0,1:T(8,128)} fusion(bf16[256,1024]{1,0:T(8,128)(2,1)S(1)} %all_gather.21, bf16[1024,3584]{1,0:T(8,128)(2,1)} %param.14, bf16[1024,3584]{1,0:T(8,128)(2,1)} %param.13, bf16[1024,3584]{1,0:T(8,128)(2,1)} %param.11, bf16[1024,3584]{1,0:T(8,128)(2,1)} %param.10), kind=kOutput, calls=%fused_computation.8 | convolution fusion | flops 7633633280 | bytes 44564480 | tf_op jit(solution)/shard_map/dot_general | solution.py:19
  36.5 15.0 %copy.32 = f32[256,14336]{1,0:T(8,128)} copy(f32[256,14336]{0,1:T(8,128)} %fusion.8) | data formatting | bytes 29360128
  51.5 237.6 %reduce-scatter.10.cloned.1.call-done = f32[32,14336]{1,0:T(8,128)} async-done(((f32[256,14336]{1,0:T(8,128)}), f32[32,14336]{1,0:T(8,128)}) %reduce-scatter.10.cloned.1.call-update) | async-done | bytes 1835024 | tf_op jit(solution)/shard_map/reduce_scatter | solution.py:41
  289.1 2.4 multiply_convert_fusion
  291.6 0.7 all-gather.5.cloned.1.call-update
  292.3 45.0 %all-gather.7.cloned.1.call-done = bf16[256,3584]{1,0:T(8,128)(2,1)} async-done(((bf16[32,3584]{1,0:T(8,128)(2,1)}), bf16[256,3584]{1,0:T(8,128)(2,1)}) %all-gather.7.cloned.1.call-update) | async-done | bytes 1835024 | tf_op jit(solution)/shard_map/all_gather | solution.py:51
  337.4 5.7 fusion.26
  343.1 42.2 %all-gather.5.cloned.1.call-done = bf16[256,3584]{1,0:T(8,128)(2,1)} async-done(((bf16[32,3584]{1,0:T(8,128)(2,1)}), bf16[256,3584]{1,0:T(8,128)(2,1)}) %all-gather.5.cloned.1.call-update) | async-done | bytes 1835024 | tf_op jit(solution)/shard_map/all_gather | solution.py:50
  385.3 5.8 fusion.25
  391.1 5.4 convolution_add_fusion.1
  396.5 1.5 pad_maximum_fusion.1
  398.0 30.0 %reduce-scatter.8.cloned.1.call-done = f32[64,2048]{1,0:T(8,128)} async-done(((f32[256,2048]{1,0:T(8,128)}), f32[64,2048]{1,0:T(8,128)}) %reduce-scatter.8.cloned.1.call-update) | async-done | bytes 524304 | tf_op jit(solution)/shard_map/reduce_scatter | solution.py:57
  428.0 1.1 fusion.23
  429.1 6.6 all_gather.24
  435.7 7.4 %all_gather.25 = bf16[256,1024]{1,0:T(8,128)(2,1)S(1)} all-gather(bf16[64,1024]{1,0:T(8,128)(2,1)S(1)} %get-tuple-element.17), channel_id=1, replica_groups=mesh['gx'=8,'gy'=4] {'gy'}, dimensions={0}, use_global_device_ids=true | all-gather | bytes 655360 | tf_op jit(solution)/shard_map/all_gather | solution.py:64
  443.1 5.3 fusion.28
  448.5 5.3 fusion.27
  453.8 2.1 convolution_add_fusion
  456.0 3.5 pad_maximum_fusion
  459.6 133.5 %reduce-scatter.12.cloned.1.call-done = f32[32,7168]{1,0:T(8,128)} async-done(((f32[256,7168]{1,0:T(8,128)}), f32[32,7168]{1,0:T(8,128)}) %reduce-scatter.12.cloned.1.call-update) | async-done | bytes 917520 | tf_op jit(solution)/shard_map/reduce_scatter | solution.py:73
  593.1 2.3 add_convert_fusion.1
  595.5 0.3 all-gather.11.cloned.1.call-start
  595.8 0.5 all-gather.11.cloned.1.call-update
  596.3 3.6 fusion.29
  599.9 6.7 add_convert_fusion
  606.6 34.7 %all-gather.9.cloned.1.call-done = bf16[256,3584]{1,0:T(8,128)(2,1)} async-done(((bf16[32,3584]{1,0:T(8,128)(2,1)}), bf16[256,3584]{1,0:T(8,128)(2,1)}) %all-gather.9.cloned.1.call-update) | async-done | bytes 1835024 | tf_op jit(solution)/shard_map/all_gather | solution.py:83
  641.2 6.7 fusion.11
  647.9 9.9 %copy.30 = bf16[1024,3584]{1,0:T(8,128)(2,1)} copy(bf16[1024,3584]{0,1:T(8,128)(2,1)} %fusion.11) | data formatting | bytes 14680064
  657.8 30.7 %all-gather.11.cloned.1.call-done = bf16[256,3584]{1,0:T(8,128)(2,1)} async-done(((bf16[32,3584]{1,0:T(8,128)(2,1)}), bf16[256,3584]{1,0:T(8,128)(2,1)}) %all-gather.11.cloned.1.call-update) | async-done | bytes 1835024 | tf_op jit(solution)/shard_map/all_gather | solution.py:84
  688.6 6.6 fusion.12
  695.1 9.9 %copy.31 = bf16[1024,3584]{1,0:T(8,128)(2,1)} copy(bf16[1024,3584]{0,1:T(8,128)(2,1)} %fusion.12) | data formatting | bytes 14680064
  (22 shorter events, 0.4 us)
Async XLA Ops:
  7.2 281.9 %reduce-scatter.10.cloned.1.call-start = ((), (), s32[]{:S(2)}) async-start(), calls=%async_computation.8 | async-start | bytes 16515072 | tf_op jit(solution)/shard_map/reduce_scatter | solution.py:41
  51.5 285.9 %all-gather.7.cloned.1.call-start = ((), (), s32[]{:S(2)}) async-start(), calls=%async_computation.4 | async-start | bytes 2064384 | tf_op jit(solution)/shard_map/all_gather | solution.py:51
  291.6 93.7 %all-gather.5.cloned.1.call-start = ((), (), s32[]{:S(2)}) async-start(), calls=%async_computation.3 | async-start | bytes 2064384 | tf_op jit(solution)/shard_map/all_gather | solution.py:50
  292.3 135.7 %reduce-scatter.8.cloned.1.call-start = ((), (), s32[]{:S(2)}) async-start(), calls=%async_computation.5 | async-start | bytes 2621440 | tf_op jit(solution)/shard_map/reduce_scatter | solution.py:57
  385.3 5.8 copy-start.1
  391.1 36.9 %copy-start.2 = (bf16[64,1024]{1,0:T(8,128)(2,1)S(1)}, bf16[64,1024]{1,0:T(8,128)(2,1)}, u32[]{:S(2)}) copy-start(bf16[64,1024]{1,0:T(8,128)(2,1)} %param.9) | copy-start | bytes 393220
  398.0 195.2 %reduce-scatter.12.cloned.1.call-start = ((), (), s32[]{:S(2)}) async-start(), calls=%async_computation.9 | async-start | bytes 8257536 | tf_op jit(solution)/shard_map/reduce_scatter | solution.py:73
  443.1 10.7 %slice-start = ((s8[7340032]{0:T(1024)(128)(4,1)}), s8[4194304]{0:T(1024)(128)(4,1)S(1)}, s32[]{:S(2)}) async-start(s8[7340032]{0:T(1024)(128)(4,1)} %bitcast.29), calls=%async_computation.10 | async-start | bytes 8388608
  448.5 5.4 slice-start.1
  459.5 133.6 %copy-start = (f32[32,14336]{1,0:T(8,128)S(1)}, f32[32,14336]{1,0:T(8,128)}, u32[]{:S(2)}) copy-start(f32[32,14336]{1,0:T(8,128)} %reduce-scatter.10.cloned.1.call-done) | copy-start | bytes 5505028
  459.6 181.7 %all-gather.9.cloned.1.call-start = ((), (), s32[]{:S(2)}) async-start(), calls=%async_computation.6 | async-start | bytes 2064384 | tf_op jit(solution)/shard_map/all_gather | solution.py:83
  595.5 93.1 %all-gather.11.cloned.1.call-start = ((), (), s32[]{:S(2)}) async-start(), calls=%async_computation.7 | async-start | bytes 2064384 | tf_op jit(solution)/shard_map/all_gather | solution.py:84
Sparse Core Ops, SparseCore 0:
  51.6 237.4 reduce-scatter.9
  291.9 45.4 all-gather.6
  340.1 45.0 all-gather.4
  398.1 29.8 reduce-scatter.7
  459.7 133.4 reduce-scatter.11
  595.8 45.4 all-gather.8
  643.4 45.0 all-gather.10
where the time goes:
time: 713 us; the launch traced here: 712 us
  waiting for transfers between devices  555 us (78%)
  matrix products  73.6 us (10%)
  local copies, waits for them, and re-layouts  34.9 us (5%)
  blocking collectives  22.9 us (3%)
  between operations  14.2 us (2%)
  other arithmetic  10.9 us (2%)
    reduce_scatter x1, waiting for transfers between devices, body(): lax.psum_scatter(matmul(rows, w_joined), 'gx', scatter_dimension=0, tiled...  238 us
    reduce_scatter x1, waiting for transfers between devices, body(): lax.psum_scatter(jnp.concatenate([back, back_dot], 1), 'gx', scatter_dime...  134 us
    all_gather x1, waiting for transfers between devices, body(): lax.all_gather(hidden_dot, 'gx', axis=0, tiled=True)  45 us
    all_gather x1, waiting for transfers between devices, body(): lax.all_gather(hidden, 'gx', axis=0, tiled=True)  42.2 us
    dot_general x4, matrix products, matmul(): return jnp.dot(left, right, preferred_element_type=jnp.float32)  37.3 us
    unnamed x13, local copies, waits for them, and re-layouts  34.9 us
    all_gather x1, waiting for transfers between devices, body(): lax.all_gather(gate_in, 'gx', axis=0, tiled=True)  34.7 us
    all_gather x1, waiting for transfers between devices, body(): lax.all_gather(upper_in, 'gx', axis=0, tiled=True)  30.7 us
  transfers between devices with their start and end apart: 7, of which 7 were waited for; matrix products, arithmetic and copies ran while one was open for 5% of the time, Pallas kernels for 0%

commit v1 on v0

v1 whole, which is shorter than its diff:
```python
import functools
import math

import jax
import jax.numpy as jnp
from jax import lax
from jax.experimental import pallas as pl
from jax.experimental.pallas import tpu as pltpu
from jax.sharding import PartitionSpec as P

TOKENS = 256


def silu_parts(gate):
    sig = jax.nn.sigmoid(gate)
    first = sig * (1.0 + gate * (1.0 - sig))
    second = sig * (1.0 - sig) * (2.0 + gate * (1.0 - 2.0 * sig))
    return (gate * sig, first, second)


def matmul(left, right):
    return jnp.dot(left, right, preferred_element_type=jnp.float32)


def lead_dot(left, right):
    return lax.dot_general(
        left, right, (((0,), (0,)), ((), ())), preferred_element_type=jnp.float32
    )


def tail_dot(left, right):
    return lax.dot_general(
        left, right, (((1,), (1,)), ((), ())), preferred_element_type=jnp.float32
    )


def gather_kernel(axis, count, arrays, *refs):
    blocks, fulls = refs[:arrays], refs[arrays : 2 * arrays]
    own_sem, send, recv = refs[2 * arrays :]
    pairs = count // 2
    me = lax.axis_index(axis)
    side = lax.rem(me, 2)
    pair = lax.div(me, 2)
    partner = me + 1 - 2 * side
    peers = [lax.rem(pair + step, pairs) * 2 + side for step in range(1, pairs)]
    sources = [lax.rem(pair + pairs - step, pairs) * 2 + side for step in range(1, pairs)]
    rows = blocks[0].shape[0]

    def place(full, index):
        return full.at[pl.ds(pl.multiple_of(index * rows, rows), rows)]

    barrier = pltpu.get_barrier_semaphore()
    for peer in [partner, *peers]:
        pl.semaphore_signal(
            barrier, inc=1, device_id={axis: peer}, device_id_type=pl.DeviceIdType.MESH
        )
    pl.semaphore_wait(barrier, pairs)

    def remote(src, full, index, peer, slot):
        return pltpu.make_async_remote_copy(
            src_ref=src,
            dst_ref=place(full, index),
            send_sem=send.at[slot],
            recv_sem=recv.at[slot],
            device_id={axis: peer},
            device_id_type=pl.DeviceIdType.MESH,
        )

    slots = 2 * pairs - 1
    direct, final, own = {}, [], []
    for i in range(arrays):
        for step, peer in enumerate(peers):
            direct[i, step] = remote(blocks[i], fulls[i], me, peer, i * slots + step)
            direct[i, step].start()
        copy = remote(blocks[i], fulls[i], me, partner, i * slots + pairs - 1)
        copy.start()
        final.append(copy)
        own.append(pltpu.make_async_copy(blocks[i], place(fulls[i], me), own_sem.at[i]))
        own[-1].start()
    for i in range(arrays):
        for step, source in enumerate(sources):
            direct[i, step].wait_recv()
            copy = remote(
                place(fulls[i], source), fulls[i], source, partner, i * slots + pairs + step
            )
            copy.start()
            final.append(copy)
    for copy in direct.values():
        copy.wait_send()
    for copy in final + own:
        copy.wait()


def gather(blocks, axis, collective_id):
    count = lax.axis_size(axis)
    arrays = len(blocks)
    slots = arrays * (count - 1)
    sent = sum(block.size * 2 * (count - 1) for block in blocks)
    return pl.pallas_call(
        functools.partial(gather_kernel, axis, count, arrays),
        out_shape=[
            jax.ShapeDtypeStruct((count * block.shape[0], block.shape[1]), block.dtype)
            for block in blocks
        ],
        in_specs=[pl.BlockSpec(memory_space=pltpu.VMEM)] * arrays,
        out_specs=[pl.BlockSpec(memory_space=pl.ANY)] * arrays,
        scratch_shapes=[
            pltpu.SemaphoreType.DMA((arrays,)),
            pltpu.SemaphoreType.DMA((slots,)),
            pltpu.SemaphoreType.DMA((slots,)),
        ],
        compiler_params=pltpu.CompilerParams(
            collective_id=collective_id, has_side_effects=True
        ),
        cost_estimate=pl.CostEstimate(
            flops=0, bytes_accessed=16 * sent, transcendentals=0
        ),
    )(*blocks)


def products_kernel(turned, gate, upper, out_gate, out_up):
    out_gate[...] = matmul(turned[...], gate[...]).astype(out_gate.dtype)
    out_up[...] = matmul(turned[...], upper[...]).astype(out_up.dtype)


def weight_products(turned, gate, upper):
    rows, depth = turned.shape
    width = gate.shape[1]
    tile = next(size for size in (512, 256, 128) if width % size == 0)
    return pl.pallas_call(
        products_kernel,
        grid=(width // tile,),
        in_specs=[
            pl.BlockSpec((rows, depth), lambda i: (0, 0)),
            pl.BlockSpec((depth, tile), lambda i: (0, i)),
            pl.BlockSpec((depth, tile), lambda i: (0, i)),
        ],
        out_specs=[pl.BlockSpec((rows, tile), lambda i: (0, i))] * 2,
        out_shape=[jax.ShapeDtypeStruct((rows, width), jnp.bfloat16)] * 2,
        cost_estimate=pl.CostEstimate(
            flops=4 * rows * depth * width,
            bytes_accessed=4 * (rows + depth) * width,
            transcendentals=0,
        ),
    )(turned, gate, upper)


def scatter_kernel(axis, count, arrays, *refs):
    parts, outs = refs[:arrays], refs[arrays : 2 * arrays]
    landed, held, got, send1, recv1, send2, recv2 = refs[2 * arrays :]
    pairs = count // 2
    me = lax.axis_index(axis)
    side = lax.rem(me, 2)
    pair = lax.div(me, 2)
    partner = me + 1 - 2 * side
    targets = [lax.rem(pair + step, pairs) * 2 for step in range(1, pairs)]
    peers = [target + side for target in targets]

    barrier = pltpu.get_barrier_semaphore()
    for peer in [partner, *peers]:
        pl.semaphore_signal(
            barrier, inc=1, device_id={axis: peer}, device_id_type=pl.DeviceIdType.MESH
        )
    pl.semaphore_wait(barrier, pairs)

    first = {}
    for i in range(arrays):
        for k, target in enumerate([*targets, pair * 2]):
            first[i, k] = pltpu.make_async_remote_copy(
                src_ref=parts[i].at[target + 1 - side],
                dst_ref=landed.at[i, k],
                send_sem=send1.at[i * pairs + k],
                recv_sem=recv1.at[i * pairs + k],
                device_id={axis: partner},
                device_id_type=pl.DeviceIdType.MESH,
            )
            first[i, k].start()
    second = {}
    for i in range(arrays):
        for k, target in enumerate([*targets, pair * 2]):
            first[i, k].wait_recv()
            term = parts[i][target + side].astype(jnp.float32) + landed[i, k].astype(jnp.float32)
            if k == pairs - 1:
                outs[i][...] = term
                continue
            held[i, k] = term.astype(held.dtype)
            second[i, k] = pltpu.make_async_remote_copy(
                src_ref=held.at[i, k],
                dst_ref=got.at[i, k],
                send_sem=send2.at[i * pairs + k],
                recv_sem=recv2.at[i * pairs + k],
                device_id={axis: peers[k]},
                device_id_type=pl.DeviceIdType.MESH,
            )
            second[i, k].start()
    for i in range(arrays):
        for k in range(pairs - 1):
            second[i, k].wait_recv()
            outs[i][...] += got[i, k].astype(jnp.float32)
    for copy in [*first.values(), *second.values()]:
        copy.wait_send()


def scatter_sum(partials, axis, collective_id):
    count = lax.axis_size(axis)
    pairs = count // 2
    arrays = len(partials)
    rows, columns = partials[0].shape[0] // count, partials[0].shape[1]
    parts = [p.astype(jnp.bfloat16).reshape(count, rows, columns) for p in partials]
    sent = 2 * rows * columns * arrays * (count - 1)
    return pl.pallas_call(
        functools.partial(scatter_kernel, axis, count, arrays),
        out_shape=[jax.ShapeDtypeStruct((rows, columns), jnp.float32)] * arrays,
        in_specs=[pl.BlockSpec(memory_space=pltpu.VMEM)] * arrays,
        out_specs=[pl.BlockSpec(memory_space=pltpu.VMEM)] * arrays,
        scratch_shapes=[
            pltpu.VMEM((arrays, pairs, rows, columns), jnp.bfloat16),
            pltpu.VMEM((arrays, max(pairs - 1, 1), rows, columns), jnp.bfloat16),
            pltpu.VMEM((arrays, max(pairs - 1, 1), rows, columns), jnp.bfloat16),
            *[pltpu.SemaphoreType.DMA((arrays * pairs,))] * 4,
        ],
        compiler_params=pltpu.CompilerParams(
            collective_id=collective_id, has_side_effects=True
        ),
        cost_estimate=pl.CostEstimate(flops=0, bytes_accessed=16 * sent, transcendentals=0),
    )(*parts)


def body(tokens, target, w_gate, w_up, w_down, t_gate, t_up, t_down):
    scale = 1.0 / math.sqrt(TOKENS)
    (xfull,) = gather([tokens], "gy", 0)
    rows = xfull
    gate, upper, gate_dot, upper_dot = scatter_sum(
        [matmul(rows, w) for w in (w_gate, w_up, t_gate, t_up)], "gx", 4
    )
    silu_val, first, second = silu_parts(gate)
    hidden = (silu_val * upper).astype(jnp.bfloat16)
    hidden_dot = (first * gate_dot * upper + silu_val * upper_dot).astype(jnp.bfloat16)
    hid_full, hid_dot_full = gather([hidden, hidden_dot], "gx", 1)
    rows = hid_full
    rows_dot = hid_dot_full
    output = matmul(rows, w_down)
    output_dot = matmul(rows_dot, w_down) + matmul(rows, t_down)
    output, output_dot = scatter_sum([output, output_dot], "gy", 6)
    grad = ((output - target.astype(jnp.float32)) * scale).astype(jnp.bfloat16)
    grad_dot = (output_dot * scale).astype(jnp.bfloat16)
    grad_full, grad_dot_full = gather([grad, grad_dot], "gy", 2)
    hvp_down = (lead_dot(hid_dot_full, grad_full) + lead_dot(hid_full, grad_dot_full)).astype(
        jnp.bfloat16
    )
    rows = grad_full
    rows_dot = grad_dot_full
    back = tail_dot(rows, w_down)
    back_dot = tail_dot(rows_dot, w_down) + tail_dot(rows, t_down)
    back, back_dot = scatter_sum([back, back_dot], "gx", 5)
    gate_in = (
        back_dot * upper * first + back * upper_dot * first + back * upper * second * gate_dot
    ).astype(jnp.bfloat16)
    upper_in = (back_dot * silu_val + back * first * gate_dot).astype(jnp.bfloat16)
    gate_full, upper_full = gather([gate_in, upper_in], "gx", 3)
    hvp_gate, hvp_up = weight_products(lax.optimization_barrier(xfull.T), gate_full, upper_full)
    return (hvp_gate, hvp_up, hvp_down)


def solution(mesh):
    return jax.shard_map(
        body,
        mesh=mesh,
        in_specs=(
            P("gy", "gx"),
            P("gy", "gx"),
            P("gx", "gy"),
            P("gx", "gy"),
            P("gy", "gx"),
            P("gx", "gy"),
            P("gx", "gy"),
            P("gy", "gx"),
        ),
        out_specs=(P("gx", "gy"), P("gx", "gy"), P("gy", "gx")),
        check_vma=False,
    )
```

time: 713 us -> 364 us (0.51)
  waiting for transfers between devices: 555 us -> 0 us
  Pallas kernels: 0 us -> 296 us
  local copies, waits for them, and re-layouts: 34.9 us -> 1.12 us
  blocking collectives: 22.9 us -> 0 us
  matrix products: 73.6 us -> 57.1 us
  between operations: 14.2 us -> 0.91 us
    reduce_scatter x3 -> x0, waiting for transfers between devices: 401 us -> none  [the longest x1 238 us: body(): lax.psum_scatter(matmul(rows, w_joined), 'gx', scatter_dimension=0, tiled...]
    pallas_call x0 -> x8, Pallas kernels: none -> 296 us  [the longest x3 165 us: scatter_sum(): pl.pallas_call(functools.partial(scatter_kernel, axis, count, arrays), ou...]
    all_gather x4 -> x0, waiting for transfers between devices: 153 us -> none  [the longest x1 45 us: body(): lax.all_gather(hidden_dot, 'gx', axis=0, tiled=True)]
    unnamed x13 -> x38, local copies, waits for them, and re-layouts: 34.9 us -> 0.1 us
    all_gather x3 -> x0, blocking collectives: 22.9 us -> none  [the longest x1 8.86 us: body(): xfull = lax.all_gather(tokens, 'gy', axis=0, tiled=True)]
    dot_general x4 -> x2, matrix products: 23.5 us -> 9.94 us  [lead_dot(): lax.dot_general(left, right, (((0,), (0,)), ((), ())), preferred_element_...]
    dot_general x4 -> x7, matrix products: 37.3 us -> 31.8 us  [matmul(): return jnp.dot(left, right, preferred_element_type=jnp.float32)]
  transfers between devices with their start and end apart: 7 -> 0, of which waited for: 7 -> 0; matrix products, arithmetic and copies ran while one was open for 5% -> 0% of each run, Pallas kernels for 0% -> 0%
where the time goes in v1:
time: 364 us; the launch traced here: 361 us
  Pallas kernels  296 us (81%)
  matrix products  57.1 us (16%)
  other arithmetic  6.57 us (2%)
    pallas_call x3, Pallas kernels, scatter_sum(): pl.pallas_call(functools.partial(scatter_kernel, axis, count, arrays), ou...  165 us
    pallas_call x4, Pallas kernels, gather(): pl.pallas_call(functools.partial(gather_kernel, axis, count, arrays), out...  121 us
    dot_general x7, matrix products, matmul(): return jnp.dot(left, right, preferred_element_type=jnp.float32)  31.8 us
    dot_general x3, matrix products, tail_dot(): lax.dot_general(left, right, (((1,), (1,)), ((), ())), preferred_element_...  15.4 us
    dot_general x2, matrix products, lead_dot(): lax.dot_general(left, right, (((0,), (0,)), ((), ())), preferred_element_...  9.94 us
    pallas_call x1, Pallas kernels, weight_products(): pl.pallas_call(products_kernel, grid=(width // tile,), in_specs=[pl.Block...  9.41 us

profile of v1, /device:TPU:0, one launch (start us, length us, event | category | flops | bytes accessed | tf_op | source)
XLA Modules:
  0.0 361.4 jit_solution(17400156778490045076)
XLA Ops:
  0.6 9.5 %shard_map.103 = bf16[256,1024]{1,0:T(8,128)(2,1)} custom-call(bf16[64,1024]{1,0:T(8,128)(2,1)} %refs_0_.1), custom_call_target="tpu_custom_call" | custom-call | bytes 6291456 | tf_op jit(solution)/shard_map/pallas_call | solution.py:99
  10.2 0.0 copy-start.1
  10.2 0.0 copy-start.10
  10.2 0.0 slice-start
  10.2 6.7 %convolution_convert_fusion.4 = bf16[256,3584]{1,0:T(8,128)(2,1)} fusion(bf16[256,1024]{1,0:T(8,128)(2,1)} %shard_map.103, bf16[1024,3584]{1,0:T(8,128)(2,1)} %param.10), kind=kOutput, calls=%fused_computation.6 | convolution fusion | flops 1879965696 | bytes 9699328 | tf_op jit(solution)/shard_map/dot_general | solution.py:22
  16.9 0.0 slice-start.2
  16.9 3.3 convolution_convert_fusion.3
  20.2 3.3 convolution_convert_fusion.2
  23.5 3.3 convolution_convert_fusion.1
  26.9 95.7 %shard_map.104 = (f32[32,3584]{1,0:T(8,128)}, f32[32,3584]{1,0:T(8,128)}, f32[32,3584]{1,0:T(8,128)}, f32[32,3584]{1,0:T(8,128)}) custom-call(bf16[8,32,3584]{2,1,0:T(8,128)(2,1)} %bitcast.33, bf16[8,32,3584]{2,1,0:T(8,128)(2,1)} %bitcast.34, bf16[8,32,3584]{2,1,0:T(8,128)(2,1)} %bitcast.35, bf16[8,32,3584]{2,1,0:T(8,128)(2,1)} %bitcast.36), custom_call_target="tpu_custom_call" | custom-call | bytes 102760448 | tf_op jit(solution)/shard_map/pallas_call | solution.py:211
  122.5 2.4 add_convert_fusion.2
  125.0 50.5 %shard_map.105 = (bf16[256,3584]{1,0:T(8,128)(2,1)}, bf16[256,3584]{1,0:T(8,128)(2,1)}) custom-call(bf16[32,3584]{1,0:T(8,128)(2,1)} %get-tuple-element.38.refs_0_, bf16[32,3584]{1,0:T(8,128)(2,1)} %get-tuple-element.37.refs_1_), custom_call_target="tpu_custom_call" | custom-call | bytes 51380224 | tf_op jit(solution)/shard_map/pallas_call | solution.py:99
  175.5 0.0 slice-start.4
  175.5 5.8 %fusion.10 = f32[256,1024]{1,0:T(8,128)S(1)} fusion(bf16[256,3584]{1,0:T(8,128)(2,1)} %get-tuple-element.24, bf16[3584,1024]{1,0:T(8,128)(2,1)} %param.12), kind=kOutput, calls=%fused_computation.27 | convolution fusion | flops 1879048192 | bytes 10223616 | tf_op jit(solution)/shard_map/dot_general | solution.py:22
  181.4 0.0 copy-done.2
  181.4 0.0 slice-start.5
  181.4 6.3 %fusion.1 = bf16[256,1024]{1,0:T(8,128)(2,1)} fusion(f32[256,1024]{1,0:T(8,128)S(1)} %fusion.10, bf16[256,3584]{1,0:T(8,128)(2,1)S(1)} %copy-done.2, bf16[3584,1024]{1,0:T(8,128)(2,1)} %param.15), kind=kOutput, calls=%fused_computation.9 | convolution fusion | flops 1879572480 | bytes 10747904 | tf_op jit(solution)/shard_map/dot_general | solution.py:22
  187.7 3.0 convolution_convert_fusion.5
  190.7 11.5 %shard_map.106 = (f32[64,1024]{1,0:T(8,128)}, f32[64,1024]{1,0:T(8,128)}) custom-call(bf16[4,64,1024]{2,1,0:T(8,128)(2,1)} %bitcast.41, bf16[4,64,1024]{2,1,0:T(8,128)(2,1)} %bitcast.40), custom_call_target="tpu_custom_call" | custom-call | bytes 12582912 | tf_op jit(solution)/shard_map/pallas_call | solution.py:211
  202.3 1.8 multiply_convert_fusion.1
  204.0 10.9 %shard_map.107 = (bf16[256,1024]{1,0:T(8,128)(2,1)}, bf16[256,1024]{1,0:T(8,128)(2,1)}) custom-call(bf16[64,1024]{1,0:T(8,128)(2,1)} %get-tuple-element.40.refs_0_, bf16[64,1024]{1,0:T(8,128)(2,1)} %get-tuple-element.39.refs_1_), custom_call_target="tpu_custom_call" | custom-call | bytes 12582912 | tf_op jit(solution)/shard_map/pallas_call | solution.py:99
  214.9 3.2 fusion.12
  218.2 6.7 %add_convert_fusion = bf16[3584,1024]{1,0:T(8,128)(2,1)} fusion(f32[3584,1024]{1,0:T(8,128)S(1)} %fusion.12, bf16[256,3584]{1,0:T(8,128)(2,1)} %get-tuple-element.23, bf16[256,1024]{1,0:T(8,128)(2,1)S(1)} %copy-done.8), kind=kOutput, calls=%fused_computation | convolution fusion | flops 1886388224 | bytes 24379392 | tf_op jit(solution)/shard_map/dot_general | solution.py:26
  224.9 5.4 %fusion.11 = f32[256,3584]{1,0:T(8,128)S(1)} fusion(bf16[256,1024]{1,0:T(8,128)(2,1)S(1)} %copy-done.8, bf16[3584,1024]{1,0:T(8,128)(2,1)} %param.12), kind=kOutput, calls=%fused_computation.28 | convolution fusion | flops 1879048192 | bytes 11534336 | tf_op jit(solution)/shard_map/dot_general | solution.py:32
  230.3 0.0 slice-start.7
  230.3 6.6 %fusion = bf16[256,3584]{1,0:T(8,128)(2,1)} fusion(f32[256,3584]{1,0:T(8,128)S(1)} %fusion.11, bf16[256,1024]{1,0:T(8,128)(2,1)S(1)} %copy-done.7, bf16[3584,1024]{1,0:T(8,128)(2,1)} %param.15), kind=kOutput, calls=%fused_computation.7 | convolution fusion | flops 1880883200 | bytes 13369344 | tf_op jit(solution)/shard_map/dot_general | solution.py:32
  237.0 3.3 convolution_convert_fusion
  240.3 57.8 %shard_map.108 = (f32[32,3584]{1,0:T(8,128)}, f32[32,3584]{1,0:T(8,128)}) custom-call(bf16[8,32,3584]{2,1,0:T(8,128)(2,1)} %bitcast.38, bf16[8,32,3584]{2,1,0:T(8,128)(2,1)} %bitcast.37), custom_call_target="tpu_custom_call" | custom-call | bytes 51380224 | tf_op jit(solution)/shard_map/pallas_call | solution.py:211
  298.2 2.3 add_convert_fusion.1
  300.5 50.4 %shard_map.109 = (bf16[256,3584]{1,0:T(8,128)(2,1)}, bf16[256,3584]{1,0:T(8,128)(2,1)}) custom-call(bf16[32,3584]{1,0:T(8,128)(2,1)} %get-tuple-element.36.refs_0_, bf16[32,3584]{1,0:T(8,128)(2,1)} %get-tuple-element.35.refs_1_), custom_call_target="tpu_custom_call" | custom-call | bytes 51380224 | tf_op jit(solution)/shard_map/pallas_call | solution.py:99
  350.9 1.0 copy.11
  351.9 9.4 %shard_map.110 = (bf16[1024,3584]{1,0:T(8,128)(2,1)}, bf16[1024,3584]{1,0:T(8,128)(2,1)}) custom-call(bf16[1024,256]{1,0:T(8,128)(2,1)} %bitcast.39, bf16[256,3584]{1,0:T(8,128)(2,1)} %get-tuple-element.31.gate, bf16[256,3584]{1,0:T(8,128)(2,1)} %get-tuple-element.32.upper), custom_call_target="tpu_custom_call" | custom-call | flops 3758096384 | bytes 18350080 | tf_op jit(solution)/shard_map/pallas_call | solution.py:130
  (34 shorter events, 0.1 us)
Async XLA Ops:
  10.2 6.7 %copy-start.1 = (bf16[256,1024]{1,0:T(8,128)(2,1)S(1)}, bf16[256,1024]{1,0:T(8,128)(2,1)}, u32[]{:S(2)}) copy-start(bf16[256,1024]{1,0:T(8,128)(2,1)} %shard_map.103) | copy-start | bytes 1572868
  10.2 6.7 %copy-start.10 = (bf16[1024,3584]{1,0:T(8,128)(2,1)S(1)}, bf16[1024,3584]{1,0:T(8,128)(2,1)}, u32[]{:S(2)}) copy-start(bf16[1024,3584]{1,0:T(8,128)(2,1)} %param.11) | copy-start | bytes 22020100
  10.2 10.0 %slice-start = ((s8[7340032]{0:T(1024)(128)(4,1)}), s8[4194304]{0:T(1024)(128)(4,1)S(1)}, s32[]{:S(2)}) async-start(s8[7340032]{0:T(1024)(128)(4,1)} %bitcast.42), calls=%async_computation | async-start | bytes 8388608
  16.9 3.3 slice-start.1
  16.9 6.6 %slice-start.2 = ((s8[7340032]{0:T(1024)(128)(4,1)}), s8[4194304]{0:T(1024)(128)(4,1)S(1)}, s32[]{:S(2)}) async-start(s8[7340032]{0:T(1024)(128)(4,1)} %bitcast.44), calls=%async_computation.2 | async-start | bytes 8388608
  20.2 3.3 slice-start.3
  175.5 5.9 %copy-start.2 = (bf16[256,3584]{1,0:T(8,128)(2,1)S(1)}, bf16[256,3584]{1,0:T(8,128)(2,1)}, u32[]{:S(2)}) copy-start(bf16[256,3584]{1,0:T(8,128)(2,1)} %get-tuple-element.23) | copy-start | bytes 5505028
  175.5 12.2 %slice-start.4 = ((s8[7340032]{0:T(1024)(128)(4,1)}), s8[4194304]{0:T(1024)(128)(4,1)S(1)}, s32[]{:S(2)}) async-start(s8[7340032]{0:T(1024)(128)(4,1)} %bitcast.46), calls=%async_computation.4 | async-start | bytes 8388608
  181.4 6.3 %slice-start.5 = ((s8[7340032]{0:T(1024)(128)(4,1)}), s8[3145728]{0:T(1024)(128)(4,1)S(1)}, s32[]{:S(2)}) async-start(s8[7340032]{0:T(1024)(128)(4,1)} %bitcast.46), calls=%async_computation.5 | async-start | bytes 6291456
  187.7 14.6 %copy-start.9 = (bf16[64,1024]{1,0:T(8,128)(2,1)S(1)}, bf16[64,1024]{1,0:T(8,128)(2,1)}, u32[]{:S(2)}) copy-start(bf16[64,1024]{1,0:T(8,128)(2,1)} %param.9) | copy-start | bytes 393220
  187.7 27.2 %copy-start = (bf16[256,3584]{1,0:T(8,128)(2,1)S(1)}, bf16[256,3584]{1,0:T(8,128)(2,1)}, u32[]{:S(2)}) copy-start(bf16[256,3584]{1,0:T(8,128)(2,1)} %get-tuple-element.24) | copy-start | bytes 5505028
  214.9 3.2 copy-start.8
  224.9 5.4 %copy-start.7 = (bf16[256,1024]{1,0:T(8,128)(2,1)S(1)}, bf16[256,1024]{1,0:T(8,128)(2,1)}, u32[]{:S(2)}) copy-start(bf16[256,1024]{1,0:T(8,128)(2,1)} %get-tuple-element.27) | copy-start | bytes 1572868
  224.9 12.1 %slice-start.6 = ((s8[7340032]{0:T(1024)(128)(4,1)}), s8[4194304]{0:T(1024)(128)(4,1)S(1)}, s32[]{:S(2)}) async-start(s8[7340032]{0:T(1024)(128)(4,1)} %bitcast.48), calls=%async_computation.6 | async-start | bytes 8388608
  230.3 6.7 %slice-start.7 = ((s8[7340032]{0:T(1024)(128)(4,1)}), s8[3145728]{0:T(1024)(128)(4,1)S(1)}, s32[]{:S(2)}) async-start(s8[7340032]{0:T(1024)(128)(4,1)} %bitcast.48), calls=%async_computation.7 | async-start | bytes 6291456
  237.0 61.2 %copy-start.3 = (f32[32,3584]{1,0:T(8,128)S(1)}, f32[32,3584]{1,0:T(8,128)}, u32[]{:S(2)}) copy-start(f32[32,3584]{1,0:T(8,128)} %get-tuple-element.19) | copy-start | bytes 1376260
  237.0 61.2 %copy-start.4 = (f32[32,3584]{1,0:T(8,128)S(1)}, f32[32,3584]{1,0:T(8,128)}, u32[]{:S(2)}) copy-start(f32[32,3584]{1,0:T(8,128)} %get-tuple-element.20) | copy-start | bytes 1376260
  237.0 61.2 %copy-start.5 = (f32[32,3584]{1,0:T(8,128)S(1)}, f32[32,3584]{1,0:T(8,128)}, u32[]{:S(2)}) copy-start(f32[32,3584]{1,0:T(8,128)} %get-tuple-element.21) | copy-start | bytes 1376260
  237.0 61.2 %copy-start.6 = (f32[32,3584]{1,0:T(8,128)S(1)}, f32[32,3584]{1,0:T(8,128)}, u32[]{:S(2)}) copy-start(f32[32,3584]{1,0:T(8,128)} %get-tuple-element.22) | copy-start | bytes 1376260
